TPU v7x, 32 devices: a whole 2x2x4 slice. The times are simulated.
32 devices in a mesh: rows: 8 (over z, y), grp: 4 (over x, core).
Axes of the slice: x: 2, y: 2, z: 4, core: 2. Of those that a mesh axis runs over, the one named last changes fastest.
Arguments:
- basis: float32 [32, 65536], P(None, ('rows', 'grp')), may hold values from -0.03125 to 0.03125, as said below
- core: float32 [32, 32], replicated, may hold values from -0.3 to 4
- snapshots: bfloat16 [4, 32, 65536], P(None, 'grp', 'rows'), may hold values from -16 to 16
Outputs:
- new_basis: float32 [32, 65536], P(None, ('rows', 'grp'))
- new_core: float32 [32, 32], replicated
- first_coeffs: float32 [4, 32, 32], replicated
Inputs may be any that keep to these rules, and one draw needn't show every extreme that they name: `basis`: rows orthonormal up to float32 rounding.
All inputs are finite; a program needn't handle non-finite values.
Results may differ from a plain program's by a relative error of at most 0.0003.
Values may be sent and summed in bfloat16 or wider, within the bound.
A program may use at most 64 MiB of HBM per device.

v0:
```python
import jax
import jax.numpy as jnp
from jax import lax
from jax.sharding import PartitionSpec as P

BATCHES = 4
epsilon = 1e-06


def contract_rows(left, right):
    return lax.dot_general(
        left,
        right,
        (((1,), (1,)), ((), ())),
        precision=lax.Precision.HIGHEST,
        preferred_element_type=jnp.float32,
    )


def matmul(left, right):
    return jnp.dot(left, right, precision=lax.Precision.HIGHEST, preferred_element_type=jnp.float32)


def lower_solve(factor, right):
    return lax.linalg.triangular_solve(factor, right, left_side=True, lower=True)


def small_update(core_now, total, lower):
    rank = core_now.shape[0]
    cols = lower.shape[0]
    top = jnp.concatenate([core_now, total], axis=1)
    bottom = jnp.concatenate([jnp.zeros((cols, rank), jnp.float32), lower.T], axis=1)
    stacked = jnp.concatenate([top, bottom], axis=0)
    moment = matmul(stacked, stacked.T)
    leading = moment[:, :rank]
    factor = jnp.linalg.cholesky(matmul(leading.T, leading))
    rotation = lower_solve(factor, leading.T).T
    fresh_core = jnp.linalg.cholesky(matmul(rotation.T, matmul(moment, rotation)))
    return (rotation, fresh_core)


def body(basis, core, snapshots):
    rank = basis.shape[0]
    basis_now = basis
    core_now = core
    firsts = []
    gram_basis = lax.psum(contract_rows(basis_now, basis_now), ("rows", "grp"))
    for batch in range(BATCHES):
        columns = lax.all_to_all(snapshots[batch], "grp", split_axis=1, concat_axis=0, tiled=True)
        raw = columns.astype(jnp.float32)
        raw_cross, raw_gram = lax.psum(
            (contract_rows(basis_now, raw), contract_rows(raw, raw)), ("rows", "grp")
        )
        inverse = lax.rsqrt(jnp.diagonal(raw_gram) + epsilon)
        scaled = raw * inverse[:, None]
        cross = raw_cross * inverse[None, :]
        gram_raw = raw_gram * inverse[:, None] * inverse[None, :]
        second = cross - matmul(gram_basis, cross)
        total = cross + second
        basis_cross = cross - matmul(gram_basis, total)
        gram = (
            gram_raw
            - matmul(total.T, cross)
            - matmul(cross.T, total)
            + matmul(total.T, matmul(gram_basis, total))
        )
        twice = scaled - matmul(total.T, basis_now)
        lower = jnp.linalg.cholesky(gram)
        fresh = lower_solve(lower, twice)
        rotation, core_now = small_update(core_now, total, lower)
        cross_fresh = lower_solve(lower, basis_cross.T).T
        halfway = lower_solve(lower, gram)
        gram_fresh = lower_solve(lower, halfway.T).T
        upper_block = jnp.concatenate([gram_basis, cross_fresh], axis=1)
        lower_block = jnp.concatenate([cross_fresh.T, gram_fresh], axis=1)
        combined = jnp.concatenate([upper_block, lower_block], axis=0)
        gram_basis = matmul(rotation.T, matmul(combined, rotation))
        firsts.append(cross)
        basis_now = matmul(rotation[:rank].T, basis_now) + matmul(rotation[rank:].T, fresh)
    return (basis_now, core_now, jnp.stack(firsts, axis=0))


def solution(mesh):
    return jax.shard_map(
        body,
        mesh=mesh,
        in_specs=(P(None, ("rows", "grp")), P(), P(None, "grp", "rows")),
        out_specs=(P(None, ("rows", "grp")), P(), P()),
        check_vma=False,
    )
```

profile of v0, /device:TPU:0, one launch (start us, length us, event | category | flops | bytes accessed | tf_op | source)
XLA Modules:
  0.0 283.6 jit_solution(1562950860485663812)
XLA Ops:
  0.6 1.9 fusion.229
  2.6 4.4 %all-to-all-start = ((bf16[8,4,2048]{2,0,1:T(8,128)(2,1)}), bf16[8,4,2048]{2,0,1:T(8,128)(2,1)S(1)}, u32[]{:S(2)}, u32[]{:S(2)}) async-start(bf16[8,4,2048]{2,0,1:T(8,128)(2,1)} %bitcast), calls=%async_computation | async-start | bytes 262144 | tf_op jit(solution)/shard_map/all_to_all | solution.py:49
  7.4 4.1 %all-to-all-done = bf16[8,4,2048]{2,0,1:T(8,128)(2,1)S(1)} async-done(((bf16[8,4,2048]{2,0,1:T(8,128)(2,1)}), bf16[8,4,2048]{2,0,1:T(8,128)(2,1)S(1)}, u32[]{:S(2)}, u32[]{:S(2)}) %all-to-all-start) | async-done | bytes 131104 | tf_op jit(solution)/shard_map/all_to_all | solution.py:49
  11.6 3.3 %all-to-all-start.1 = ((bf16[8,4,2048]{2,0,1:T(8,128)(2,1)}), bf16[8,4,2048]{2,0,1:T(8,128)(2,1)S(1)}, u32[]{:S(2)}, u32[]{:S(2)}) async-start(bf16[8,4,2048]{2,0,1:T(8,128)(2,1)} %bitcast.15), calls=%async_computation.1 | async-start | bytes 262144 | tf_op jit(solution)/shard_map/all_to_all | solution.py:49
  15.3 42.1 %all-reduce.7 = (f32[32,32]{1,0:T(8,128)S(1)}, f32[32,32]{0,1:T(8,128)S(1)}, f32[32,32]{0,1:T(8,128)S(1)}) all-reduce(f32[32,32]{1,0:T(8,128)S(1)} %fusion.230, f32[32,32]{0,1:T(8,128)S(1)} %fusion.18, f32[32,32]{0,1:T(8,128)S(1)} %fusion.16), channel_id=1, replica_groups=mesh['rows'=8,'grp'=4] {'rows','grp'}, use_global_device_ids=true, to_apply=%region_2.0 | all-reduce | flops 3072 | bytes 24576 | tf_op jit(solution)/shard_map/psum | solution.py:47
  57.4 0.7 gather_fusion
  59.3 2.9 %cholesky.194 = f32[32,32]{1,0:T(8,128)S(1)} custom-call(f32[32,32]{1,0:T(8,128)S(1)} %fusion.134), custom_call_target="Cholesky" | custom-call | tf_op jit(solution)/shard_map/jit(cholesky)/cholesky | solution.py:68
  62.3 0.6 compare_reduce_fusion.11
  62.9 0.7 fusion.143
  63.6 2.4 custom-call.34
  67.2 2.9 %cholesky.205 = f32[32,32]{1,0:T(8,128)S(1)} custom-call(f32[32,32]{1,0:T(8,128)S(1)} %fusion.133), custom_call_target="Cholesky" | custom-call | tf_op jit(solution)/shard_map/jit(cholesky)/cholesky | solution.py:36
  70.1 0.6 compare_reduce_fusion.10
  70.8 0.7 fusion.64
  71.4 2.4 custom-call.33
  75.2 0.4 fusion.127
  76.0 0.4 convolution_add_fusion.3
  76.5 3.5 %all-to-all-start.2 = ((bf16[8,4,2048]{2,0,1:T(8,128)(2,1)}), bf16[8,4,2048]{2,0,1:T(8,128)(2,1)S(1)}, u32[]{:S(2)}, u32[]{:S(2)}) async-start(bf16[8,4,2048]{2,0,1:T(8,128)(2,1)} %bitcast.39), calls=%async_computation.2 | async-start | bytes 262144 | tf_op jit(solution)/shard_map/all_to_all | solution.py:49
  80.4 41.5 %all-reduce.6 = (f32[32,32]{0,1:T(8,128)S(1)}, f32[32,32]{0,1:T(8,128)S(1)}) all-reduce(f32[32,32]{0,1:T(8,128)S(1)} %fusion.14, f32[32,32]{0,1:T(8,128)S(1)} %fusion.12), channel_id=1, replica_groups=mesh['rows'=8,'grp'=4] {'rows','grp'}, use_global_device_ids=true, to_apply=%region_5.9 | all-reduce | flops 2048 | bytes 16384 | tf_op jit(solution)/shard_map/psum | solution.py:51
  121.9 0.7 gather_fusion.1
  123.5 2.9 %cholesky.216 = f32[32,32]{1,0:T(8,128)S(1)} custom-call(f32[32,32]{1,0:T(8,128)S(1)} %fusion.129), custom_call_target="Cholesky" | custom-call | tf_op jit(solution)/shard_map/jit(cholesky)/cholesky | solution.py:38
  126.6 0.6 compare_reduce_fusion.9
  127.3 0.6 fusion.163
  128.5 2.9 %cholesky.227 = f32[32,32]{1,0:T(8,128)S(1)} custom-call(f32[32,32]{1,0:T(8,128)S(1)} %fusion.121), custom_call_target="Cholesky" | custom-call | tf_op jit(solution)/shard_map/jit(cholesky)/cholesky | solution.py:68
  131.5 0.6 compare_reduce_fusion.8
  132.1 0.7 fusion.144
  132.8 2.4 custom-call.39
  136.4 2.9 %cholesky.238 = f32[32,32]{1,0:T(8,128)S(1)} custom-call(f32[32,32]{1,0:T(8,128)S(1)} %fusion.120), custom_call_target="Cholesky" | custom-call | tf_op jit(solution)/shard_map/jit(cholesky)/cholesky | solution.py:36
  139.4 0.6 compare_reduce_fusion.7
  140.0 0.7 fusion.65
  140.7 2.4 custom-call.38
  145.2 0.4 convolution_add_fusion.2
  145.7 3.5 %all-to-all-start.3 = ((bf16[8,4,2048]{2,0,1:T(8,128)(2,1)}), bf16[8,4,2048]{2,0,1:T(8,128)(2,1)S(1)}, u32[]{:S(2)}, u32[]{:S(2)}) async-start(bf16[8,4,2048]{2,0,1:T(8,128)(2,1)} %bitcast.63), calls=%async_computation.3 | async-start | bytes 262144 | tf_op jit(solution)/shard_map/all_to_all | solution.py:49
  149.7 40.7 %all-reduce.5 = (f32[32,32]{0,1:T(8,128)S(1)}, f32[32,32]{0,1:T(8,128)S(1)}) all-reduce(f32[32,32]{0,1:T(8,128)S(1)} %fusion.10, f32[32,32]{0,1:T(8,128)S(1)} %fusion.8), channel_id=1, replica_groups=mesh['rows'=8,'grp'=4] {'rows','grp'}, use_global_device_ids=true, to_apply=%region_7.12 | all-reduce | flops 2048 | bytes 16384 | tf_op jit(solution)/shard_map/psum | solution.py:51
  190.4 0.7 gather_fusion.2
  192.0 2.9 %cholesky.249 = f32[32,32]{1,0:T(8,128)S(1)} custom-call(f32[32,32]{1,0:T(8,128)S(1)} %fusion.116), custom_call_target="Cholesky" | custom-call | tf_op jit(solution)/shard_map/jit(cholesky)/cholesky | solution.py:38
  195.1 0.6 compare_reduce_fusion.6
  195.7 0.6 fusion.164
  197.0 2.9 %cholesky.260 = f32[32,32]{1,0:T(8,128)S(1)} custom-call(f32[32,32]{1,0:T(8,128)S(1)} %fusion.108), custom_call_target="Cholesky" | custom-call | tf_op jit(solution)/shard_map/jit(cholesky)/cholesky | solution.py:68
  199.9 0.6 compare_reduce_fusion.5
  200.6 0.7 fusion.142
  201.2 2.4 custom-call.44
  204.8 2.9 %cholesky.271 = f32[32,32]{1,0:T(8,128)S(1)} custom-call(f32[32,32]{1,0:T(8,128)S(1)} %fusion.107), custom_call_target="Cholesky" | custom-call | tf_op jit(solution)/shard_map/jit(cholesky)/cholesky | solution.py:36
  207.8 0.6 compare_reduce_fusion.4
  208.5 0.7 fusion.66
  209.1 2.4 custom-call.43
  213.7 0.4 convolution_add_fusion.1
  214.6 39.8 %all-reduce.4 = (f32[32,32]{0,1:T(8,128)S(1)}, f32[32,32]{0,1:T(8,128)S(1)}) all-reduce(f32[32,32]{0,1:T(8,128)S(1)} %fusion.6, f32[32,32]{0,1:T(8,128)S(1)} %fusion.4), channel_id=1, replica_groups=mesh['rows'=8,'grp'=4] {'rows','grp'}, use_global_device_ids=true, to_apply=%region_9.14 | all-reduce | flops 2048 | bytes 16384 | tf_op jit(solution)/shard_map/psum | solution.py:51
  254.5 0.7 gather_fusion.3
  256.1 2.9 %cholesky.282 = f32[32,32]{1,0:T(8,128)S(1)} custom-call(f32[32,32]{1,0:T(8,128)S(1)} %fusion.103), custom_call_target="Cholesky" | custom-call | tf_op jit(solution)/shard_map/jit(cholesky)/cholesky | solution.py:38
  259.2 0.6 compare_reduce_fusion.3
  259.9 0.6 select_select_fusion.5
  260.8 0.7 copy.105
  261.8 2.9 %cholesky.293 = f32[32,32]{1,0:T(8,128)S(1)} custom-call(f32[32,32]{1,0:T(8,128)S(1)} %fusion.95), custom_call_target="Cholesky" | custom-call | tf_op jit(solution)/shard_map/jit(cholesky)/cholesky | solution.py:68
  264.7 0.6 compare_reduce_fusion.2
  265.4 0.7 select_bitcast_fusion
  266.0 2.4 custom-call.49
  269.0 2.9 %cholesky.304 = f32[32,32]{1,0:T(8,128)S(1)} custom-call(f32[32,32]{1,0:T(8,128)S(1)} %fusion.94), custom_call_target="Cholesky" | custom-call | tf_op jit(solution)/shard_map/jit(cholesky)/cholesky | solution.py:36
  272.0 0.6 compare_reduce_fusion.1
  272.6 0.7 fusion.67
  273.3 2.4 custom-call.48
  276.5 2.9 %cholesky.315 = f32[32,32]{1,0:T(8,128)S(1)} custom-call(f32[32,32]{1,0:T(8,128)S(1)} %fusion.88), custom_call_target="Cholesky" | custom-call | tf_op jit(solution)/shard_map/jit(cholesky)/cholesky | solution.py:38
  279.4 0.6 compare_reduce_fusion
  280.1 1.3 select_select_fusion.4
  282.5 1.1 convolution_add_fusion
  (138 shorter events, 20.1 us)
Async XLA Ops:
  0.6 6.4 %copy-start = (f32[32,2048]{1,0:T(8,128)S(1)}, f32[32,2048]{1,0:T(8,128)}, u32[]{:S(2)}) copy-start(f32[32,2048]{1,0:T(8,128)} %param.10) | copy-start | bytes 786436
  2.6 4.4 %copy-start.1 = (f32[32,32]{1,0:T(8,128)S(1)}, f32[32,32]{1,0:T(8,128)}, u32[]{:S(2)}) copy-start(f32[32,32]{1,0:T(8,128)} %param.11) | copy-start | bytes 12292
  2.6 9.0 %all-to-all-start = ((bf16[8,4,2048]{2,0,1:T(8,128)(2,1)}), bf16[8,4,2048]{2,0,1:T(8,128)(2,1)S(1)}, u32[]{:S(2)}, u32[]{:S(2)}) async-start(bf16[8,4,2048]{2,0,1:T(8,128)(2,1)} %bitcast), calls=%async_computation | async-start | bytes 262144 | tf_op jit(solution)/shard_map/all_to_all | solution.py:49
  11.6 64.9 %all-to-all-start.1 = ((bf16[8,4,2048]{2,0,1:T(8,128)(2,1)}), bf16[8,4,2048]{2,0,1:T(8,128)(2,1)S(1)}, u32[]{:S(2)}, u32[]{:S(2)}) async-start(bf16[8,4,2048]{2,0,1:T(8,128)(2,1)} %bitcast.15), calls=%async_computation.1 | async-start | bytes 262144 | tf_op jit(solution)/shard_map/all_to_all | solution.py:49
  76.5 69.2 %all-to-all-start.2 = ((bf16[8,4,2048]{2,0,1:T(8,128)(2,1)}), bf16[8,4,2048]{2,0,1:T(8,128)(2,1)S(1)}, u32[]{:S(2)}, u32[]{:S(2)}) async-start(bf16[8,4,2048]{2,0,1:T(8,128)(2,1)} %bitcast.39), calls=%async_computation.2 | async-start | bytes 262144 | tf_op jit(solution)/shard_map/all_to_all | solution.py:49
  145.7 68.5 %all-to-all-start.3 = ((bf16[8,4,2048]{2,0,1:T(8,128)(2,1)}), bf16[8,4,2048]{2,0,1:T(8,128)(2,1)S(1)}, u32[]{:S(2)}, u32[]{:S(2)}) async-start(bf16[8,4,2048]{2,0,1:T(8,128)(2,1)} %bitcast.63), calls=%async_computation.3 | async-start | bytes 262144 | tf_op jit(solution)/shard_map/all_to_all | solution.py:49
where the time goes:
time: 285 us; the launch traced here: 284 us
  blocking collectives  164 us (58%)
  other arithmetic  71.8 us (25%)
  matrix products  20.3 us (7%)
  starting transfers between devices  14.7 us (5%)
  local copies, waits for them, and re-layouts  7.12 us (2%)
  waiting for transfers between devices  4.15 us (1%)
    psum x3, blocking collectives, body(): lax.psum((contract_rows(basis_now, raw), contract_rows(raw, raw)), ('rows...  122 us
    psum x1, blocking collectives, body(): gram_basis = lax.psum(contract_rows(basis_now, basis_now), ('rows', 'grp'))  42.1 us
    another operation x16, other arithmetic, lower_solve(): lax.linalg.triangular_solve(factor, right, left_side=True, lower=True)  24.7 us
    all_to_all x4, starting transfers between devices, body(): lax.all_to_all(snapshots[batch], 'grp', split_axis=1, concat_axis=0, tile...  14.7 us
    another operation x12, other arithmetic, small_update(): jnp.linalg.cholesky(matmul(rotation.T, matmul(moment, rotation)))  14.7 us
    another operation x12, other arithmetic, small_update(): factor = jnp.linalg.cholesky(matmul(leading.T, leading))  14.4 us
    another operation x12, other arithmetic, body(): lower = jnp.linalg.cholesky(gram)  14.4 us
    dot_general x54, matrix products, matmul(): jnp.dot(left, right, precision=lax.Precision.HIGHEST, preferred_element_t...  13.7 us
  transfers between devices with their start and end apart: 4, of which 1 were waited for; matrix products, arithmetic and copies ran while one was open for 24% of the time, Pallas kernels for 0%

commit v1 on v0

--- a/solution.py
+++ b/solution.py
@@ -44,7 +44,9 @@
     basis_now = basis
     core_now = core
     firsts = []
-    gram_basis = lax.psum(contract_rows(basis_now, basis_now), ("rows", "grp"))
+    gram_basis = jnp.sum(
+        lax.all_gather(contract_rows(basis_now, basis_now), ("rows", "grp")), axis=0
+    )
     for batch in range(BATCHES):
         columns = lax.all_to_all(snapshots[batch], "grp", split_axis=1, concat_axis=0, tiled=True)
         raw = columns.astype(jnp.float32)

time: 285 us -> 321 us (1.13)
  blocking collectives: 164 us -> 205 us
  waiting for transfers between devices: 4.15 us -> 0.01 us
    all_gather x0 -> x1, blocking collectives: none -> 44.4 us  [body(): lax.all_gather(contract_rows(basis_now, basis_now), ('rows', 'grp'))]
    psum x1 -> x0, blocking collectives: 42.1 us -> none  [body(): gram_basis = lax.psum(contract_rows(basis_now, basis_now), ('rows', 'grp'))]
    psum x3 -> x4, blocking collectives: 122 us -> 161 us  [body(): lax.psum((contract_rows(basis_now, raw), contract_rows(raw, raw)), ('rows...]
    all_to_all x4, waiting for transfers between devices: 4.15 us -> 0.01 us  [body(): lax.all_to_all(snapshots[batch], 'grp', split_axis=1, concat_axis=0, tile...]
  transfers between devices with their start and end apart: 4 -> 4, of which waited for: 1 -> 0; matrix products, arithmetic and copies ran while one was open for 24% -> 21% of each run, Pallas kernels for 0% -> 0%
where the time goes in v1:
time: 321 us; the launch traced here: 320 us
  blocking collectives  205 us (64%)
  other arithmetic  71.8 us (22%)
  matrix products  20.3 us (6%)
  starting transfers between devices  14.8 us (5%)
  local copies, waits for them, and re-layouts  7.12 us (2%)
    psum x4, blocking collectives, body(): lax.psum((contract_rows(basis_now, raw), contract_rows(raw, raw)), ('rows...  161 us
    all_gather x1, blocking collectives, body(): lax.all_gather(contract_rows(basis_now, basis_now), ('rows', 'grp'))  44.4 us
    another operation x16, other arithmetic, lower_solve(): lax.linalg.triangular_solve(factor, right, left_side=True, lower=True)  24.7 us
    all_to_all x4, starting transfers between devices, body(): lax.all_to_all(snapshots[batch], 'grp', split_axis=1, concat_axis=0, tile...  14.8 us
    another operation x12, other arithmetic, small_update(): jnp.linalg.cholesky(matmul(rotation.T, matmul(moment, rotation)))  14.7 us
    another operation x12, other arithmetic, small_update(): factor = jnp.linalg.cholesky(matmul(leading.T, leading))  14.4 us
    another operation x12, other arithmetic, body(): lower = jnp.linalg.cholesky(gram)  14.4 us
    dot_general x54, matrix products, matmul(): jnp.dot(left, right, precision=lax.Precision.HIGHEST, preferred_element_t...  13.7 us
  transfers between devices with their start and end apart: 4, of which 0 were waited for; matrix products, arithmetic and copies ran while one was open for 21% of the time, Pallas kernels for 0%

profile of v1, /device:TPU:0, one launch (start us, length us, event | category | flops | bytes accessed | tf_op | source)
XLA Modules:
  0.0 320.3 jit_solution(8264040308730307779)
XLA Ops:
  0.6 1.9 fusion.229
  2.6 4.4 %all-to-all-start = ((bf16[8,4,2048]{2,0,1:T(8,128)(2,1)}), bf16[8,4,2048]{2,0,1:T(8,128)(2,1)S(1)}, u32[]{:S(2)}, u32[]{:S(2)}) async-start(bf16[8,4,2048]{2,0,1:T(8,128)(2,1)} %bitcast), calls=%async_computation | async-start | bytes 262144 | tf_op jit(solution)/shard_map/all_to_all | solution.py:51
  7.4 44.4 %all-gather = f32[1024,32]{1,0:T(8,128)S(1)} all-gather(f32[32,32]{1,0:T(8,128)S(1)} %fusion.230), channel_id=2, replica_groups=mesh['rows'=8,'grp'=4] {'rows','grp'}, dimensions={0}, use_global_device_ids=true | all-gather | bytes 135168 | tf_op jit(solution)/shard_map/all_gather | solution.py:48
  51.8 3.3 %all-to-all-start.1 = ((bf16[8,4,2048]{2,0,1:T(8,128)(2,1)}), bf16[8,4,2048]{2,0,1:T(8,128)(2,1)S(1)}, u32[]{:S(2)}, u32[]{:S(2)}) async-start(bf16[8,4,2048]{2,0,1:T(8,128)(2,1)} %bitcast.16), calls=%async_computation.1 | async-start | bytes 262144 | tf_op jit(solution)/shard_map/all_to_all | solution.py:51
  55.6 37.2 %all-reduce.7 = (f32[32,32]{0,1:T(8,128)S(1)}, f32[32,32]{0,1:T(8,128)S(1)}) all-reduce(f32[32,32]{0,1:T(8,128)S(1)} %fusion.18, f32[32,32]{0,1:T(8,128)S(1)} %fusion.16), channel_id=1, replica_groups=mesh['rows'=8,'grp'=4] {'rows','grp'}, use_global_device_ids=true, to_apply=%region_0.0 | all-reduce | flops 2048 | bytes 16384 | tf_op jit(solution)/shard_map/psum | solution.py:53
  92.8 0.7 gather_fusion
  94.7 2.9 cholesky.194
  97.7 0.6 compare_reduce_fusion.11
  98.3 0.7 fusion.143
  99.0 2.4 custom-call.34
  102.6 2.9 cholesky.205
  105.5 0.6 compare_reduce_fusion.10
  106.2 0.7 fusion.64
  106.8 2.4 custom-call.33
  110.6 0.4 fusion.127
  111.4 0.4 convolution_add_fusion.3
  111.9 3.5 %all-to-all-start.2 = ((bf16[8,4,2048]{2,0,1:T(8,128)(2,1)}), bf16[8,4,2048]{2,0,1:T(8,128)(2,1)S(1)}, u32[]{:S(2)}, u32[]{:S(2)}) async-start(bf16[8,4,2048]{2,0,1:T(8,128)(2,1)} %bitcast.40), calls=%async_computation.2 | async-start | bytes 262144 | tf_op jit(solution)/shard_map/all_to_all | solution.py:51
  115.8 42.8 %all-reduce.6 = (f32[32,32]{0,1:T(8,128)S(1)}, f32[32,32]{0,1:T(8,128)S(1)}) all-reduce(f32[32,32]{0,1:T(8,128)S(1)} %fusion.14, f32[32,32]{0,1:T(8,128)S(1)} %fusion.12), channel_id=1, replica_groups=mesh['rows'=8,'grp'=4] {'rows','grp'}, use_global_device_ids=true, to_apply=%region_5.9 | all-reduce | flops 2048 | bytes 16384 | tf_op jit(solution)/shard_map/psum | solution.py:53
  158.7 0.7 gather_fusion.1
  160.2 2.9 cholesky.216
  163.4 0.6 compare_reduce_fusion.9
  164.0 0.6 fusion.163
  165.3 2.9 cholesky.227
  168.2 0.6 compare_reduce_fusion.8
  168.9 0.7 fusion.144
  169.5 2.4 custom-call.39
  173.1 2.9 cholesky.238
  176.1 0.6 compare_reduce_fusion.7
  176.7 0.7 fusion.65
  177.4 2.4 custom-call.38
  181.9 0.4 convolution_add_fusion.2
  182.4 3.5 %all-to-all-start.3 = ((bf16[8,4,2048]{2,0,1:T(8,128)(2,1)}), bf16[8,4,2048]{2,0,1:T(8,128)(2,1)S(1)}, u32[]{:S(2)}, u32[]{:S(2)}) async-start(bf16[8,4,2048]{2,0,1:T(8,128)(2,1)} %bitcast.64), calls=%async_computation.3 | async-start | bytes 262144 | tf_op jit(solution)/shard_map/all_to_all | solution.py:51
  186.4 40.1 %all-reduce.5 = (f32[32,32]{0,1:T(8,128)S(1)}, f32[32,32]{0,1:T(8,128)S(1)}) all-reduce(f32[32,32]{0,1:T(8,128)S(1)} %fusion.10, f32[32,32]{0,1:T(8,128)S(1)} %fusion.8), channel_id=1, replica_groups=mesh['rows'=8,'grp'=4] {'rows','grp'}, use_global_device_ids=true, to_apply=%region_7.12 | all-reduce | flops 2048 | bytes 16384 | tf_op jit(solution)/shard_map/psum | solution.py:53
  226.5 0.7 gather_fusion.2
  228.0 2.9 cholesky.249
  231.2 0.6 compare_reduce_fusion.6
  231.8 0.6 fusion.164
  233.1 2.9 cholesky.260
  236.0 0.6 compare_reduce_fusion.5
  236.7 0.7 fusion.142
  237.3 2.4 custom-call.44
  240.9 2.9 cholesky.271
  243.9 0.6 compare_reduce_fusion.4
  244.5 0.7 fusion.66
  245.2 2.4 custom-call.43
  249.7 0.4 convolution_add_fusion.1
  250.7 40.5 %all-reduce.4 = (f32[32,32]{0,1:T(8,128)S(1)}, f32[32,32]{0,1:T(8,128)S(1)}) all-reduce(f32[32,32]{0,1:T(8,128)S(1)} %fusion.6, f32[32,32]{0,1:T(8,128)S(1)} %fusion.4), channel_id=1, replica_groups=mesh['rows'=8,'grp'=4] {'rows','grp'}, use_global_device_ids=true, to_apply=%region_9.14 | all-reduce | flops 2048 | bytes 16384 | tf_op jit(solution)/shard_map/psum | solution.py:53
  291.2 0.7 gather_fusion.3
  292.8 2.9 cholesky.282
  295.9 0.6 compare_reduce_fusion.3
  296.6 0.6 select_select_fusion.5
  297.5 0.7 copy.105
  298.5 2.9 cholesky.293
  301.4 0.6 compare_reduce_fusion.2
  302.1 0.7 select_bitcast_fusion
  302.7 2.4 custom-call.49
  305.7 2.9 cholesky.304
  308.7 0.6 compare_reduce_fusion.1
  309.3 0.7 fusion.67
  310.0 2.4 custom-call.48
  313.2 2.9 cholesky.315
  316.1 0.6 compare_reduce_fusion
  316.8 1.3 select_select_fusion.4
  319.2 1.1 convolution_add_fusion
  (140 shorter events, 20.2 us)
Async XLA Ops:
  0.6 6.4 %copy-start = (f32[32,2048]{1,0:T(8,128)S(1)}, f32[32,2048]{1,0:T(8,128)}, u32[]{:S(2)}) copy-start(f32[32,2048]{1,0:T(8,128)} %param.10) | copy-start | bytes 786436
  2.6 4.4 %copy-start.1 = (f32[32,32]{1,0:T(8,128)S(1)}, f32[32,32]{1,0:T(8,128)}, u32[]{:S(2)}) copy-start(f32[32,32]{1,0:T(8,128)} %param.11) | copy-start | bytes 12292
  2.6 49.2 %all-to-all-start = ((bf16[8,4,2048]{2,0,1:T(8,128)(2,1)}), bf16[8,4,2048]{2,0,1:T(8,128)(2,1)S(1)}, u32[]{:S(2)}, u32[]{:S(2)}) async-start(bf16[8,4,2048]{2,0,1:T(8,128)(2,1)} %bitcast), calls=%async_computation | async-start | bytes 262144 | tf_op jit(solution)/shard_map/all_to_all | solution.py:51
  51.8 60.1 %all-to-all-start.1 = ((bf16[8,4,2048]{2,0,1:T(8,128)(2,1)}), bf16[8,4,2048]{2,0,1:T(8,128)(2,1)S(1)}, u32[]{:S(2)}, u32[]{:S(2)}) async-start(bf16[8,4,2048]{2,0,1:T(8,128)(2,1)} %bitcast.16), calls=%async_computation.1 | async-start | bytes 262144 | tf_op jit(solution)/shard_map/all_to_all | solution.py:51
  111.9 70.5 %all-to-all-start.2 = ((bf16[8,4,2048]{2,0,1:T(8,128)(2,1)}), bf16[8,4,2048]{2,0,1:T(8,128)(2,1)S(1)}, u32[]{:S(2)}, u32[]{:S(2)}) async-start(bf16[8,4,2048]{2,0,1:T(8,128)(2,1)} %bitcast.40), calls=%async_computation.2 | async-start | bytes 262144 | tf_op jit(solution)/shard_map/all_to_all | solution.py:51
  182.4 67.8 %all-to-all-start.3 = ((bf16[8,4,2048]{2,0,1:T(8,128)(2,1)}), bf16[8,4,2048]{2,0,1:T(8,128)(2,1)S(1)}, u32[]{:S(2)}, u32[]{:S(2)}) async-start(bf16[8,4,2048]{2,0,1:T(8,128)(2,1)} %bitcast.64), calls=%async_computation.3 | async-start | bytes 262144 | tf_op jit(solution)/shard_map/all_to_all | solution.py:51
